TPU v7x, 32 devices: a whole 2x2x4 slice. The times are simulated.
32 devices in a mesh: rows: 8 (over z, y), rep: 4 (over x, core).
Axes of the slice: x: 2, y: 2, z: 4, core: 2. Of those that a mesh axis runs over, the one named last changes fastest.
Arguments:
- binned: int32 [8192, 1024], P('rows', 'rep'), may hold values from 0 to 127
- gradients: bfloat16 [8192], P('rows'), may hold values from -3 to 3
- hessians: bfloat16 [8192], P('rows'), may hold values from 0.019897461 to 0.25
- parents: int32 [8192], P('rows'), may hold values from 0 to 15
- split_feature: int32 [16], replicated, may hold values from 0 to 1023
- split_bin: int32 [16], replicated, may hold values from 32 to 95
- elected: int32 [32, 512], P(None, 'rep'), may hold values from 0 to 255
Outputs:
- new_nodes: int32 [8192], P('rows')
- best_gain: float32 [32, 4, 128], P(None, 'rep', 'rows')
- node_best: float32 [32], replicated
All inputs are finite; a program needn't handle non-finite values.
Results may differ from a plain program's by a relative error of at most 0.0003.
Values sent between devices are 32-bit elements; how exact they have to be, the bound alone decides.
A program may use at most 64 MiB of HBM per device.

v0:
```python
import math

import jax
import jax.numpy as jnp
from jax import lax
from jax.sharding import PartitionSpec as P

BINS = 128


l2_penalty = 1.0


def body(binned, gradients, hessians, parents, split_feature, split_bin, elected):
    rows_here, block_width = binned.shape
    node_count, slots_here = elected.shape
    parent_count = split_feature.shape[0]
    rep_index = lax.axis_index("rep")
    parent_hot = parents[:, None] == jnp.arange(parent_count, dtype=jnp.int32)[None, :]
    row_feature = jnp.sum(jnp.where(parent_hot, split_feature[None, :], 0), axis=1)
    row_bin = jnp.sum(jnp.where(parent_hot, split_bin[None, :], 0), axis=1)
    local_col = row_feature - rep_index * block_width
    column_hot = local_col[:, None] == jnp.arange(block_width, dtype=jnp.int32)[None, :]
    owned_value = jnp.sum(jnp.where(column_hot, binned, 0), axis=1)
    owned_mask = (local_col >= 0) & (local_col < block_width)
    side_here = jnp.where(owned_mask & (owned_value > row_bin), 1, 0).astype(jnp.int32)
    side_bits = lax.pmax(side_here, "rep")
    new_nodes = 2 * parents + side_bits
    node_hot = new_nodes[:, None] == jnp.arange(node_count, dtype=jnp.int32)[None, :]
    nothing = jnp.zeros((), jnp.bfloat16)
    weights = jnp.concatenate(
        [
            jnp.where(node_hot, gradients[:, None], nothing),
            jnp.where(node_hot, hessians[:, None], nothing),
        ],
        axis=1,
    )
    feature_block = math.gcd(block_width, max(1, 8192 // BINS))
    block_count = block_width // feature_block
    row_block = math.gcd(rows_here, max(8, 2**22 // (feature_block * BINS)))
    row_count = rows_here // row_block
    bin_ids = jnp.arange(BINS, dtype=jnp.int32)
    blocks = jnp.transpose(
        binned.reshape(row_count, row_block, block_count, feature_block), (2, 0, 1, 3)
    )
    weight_blocks = weights.reshape(row_count, row_block, 2 * node_count)

    def build_block(unused, columns):

        def add_rows(total, pair):
            piece, weight_piece = pair
            one_hot = (piece[:, :, None] == bin_ids[None, None, :]).astype(jnp.bfloat16)
            one_hot = one_hot.reshape(row_block, feature_block * BINS)
            partial_value = lax.dot_general(
                weight_piece, one_hot, (((0,), (0,)), ((), ())), preferred_element_type=jnp.float32
            )
            return (total + partial_value, None)

        start = jnp.zeros((2 * node_count, feature_block * BINS), jnp.float32)
        summed_rows, _ = lax.scan(add_rows, start, (columns, weight_blocks))
        return (unused, summed_rows)

    _, block_sums = lax.scan(build_block, 0, blocks)
    block_sums = block_sums.reshape(block_count, 2, node_count, feature_block, BINS)
    block_of = (elected // feature_block)[None, :, :]
    inner_of = (elected % feature_block)[None, :, :]
    channel = jnp.arange(2, dtype=jnp.int32)[:, None, None]
    node_of = jnp.arange(node_count, dtype=jnp.int32)[None, :, None]
    selected = block_sums[block_of, channel, node_of, inner_of]
    row_devices = lax.axis_size("rows")
    owned_slots = slots_here // row_devices
    sectioned = selected.reshape(2, node_count, row_devices, owned_slots, BINS)
    arrived = lax.all_to_all(sectioned, "rows", split_axis=2, concat_axis=2, tiled=True)
    summed = jnp.sum(arrived, axis=2)
    totals = jnp.sum(summed, axis=3)
    total_grad = totals[0][:, :, None]
    total_hess = totals[1][:, :, None]
    left_sums = jnp.cumsum(summed, axis=3)[:, :, :, :-1]
    left_grad = left_sums[0]
    left_hess = left_sums[1]
    split_gain = 0.5 * (
        left_grad * left_grad / (left_hess + l2_penalty)
        + (total_grad - left_grad) ** 2 / (total_hess - left_hess + l2_penalty)
        - total_grad * total_grad / (total_hess + l2_penalty)
    )
    best_slot = jnp.max(split_gain, axis=2)
    node_local = jnp.max(best_slot, axis=1)
    node_best = lax.pmax(node_local, ("rows", "rep"))
    return (new_nodes, best_slot[:, None, :], node_best)


def solution(mesh):
    return jax.shard_map(
        body,
        mesh=mesh,
        in_specs=(P("rows", "rep"), P("rows"), P("rows"), P("rows"), P(), P(), P(None, "rep")),
        out_specs=(P("rows"), P(None, "rep", "rows"), P()),
        check_vma=False,
    )
```

profile of v0, /device:TPU:0, one launch (start us, length us, event | category | flops | bytes accessed | tf_op | source)
XLA Modules:
  0.0 422.1 jit_solution(2758746676563248309)
XLA Ops:
  0.6 1.6 copy.16
  2.2 0.8 select_reduce_fusion.1
  3.0 1.6 select_reduce_fusion
  4.6 6.4 %pmax.14 = s32[1024]{0:T(1024)S(1)} all-reduce(s32[1024]{0:T(1024)S(1)} %and_select_fusion), channel_id=1, replica_groups=mesh['rows'=8,'rep'=4] {'rep'}, use_global_device_ids=true, to_apply=%region_3.4 | all-reduce | flops 1024 | bytes 8192 | tf_op jit(solution)/shard_map/pmax | solution.py:27
  11.0 0.7 multiply_add_fusion
  11.7 0.0 copy-start.1
  11.7 0.7 broadcast_in_dim.102
  12.4 0.7 broadcast_in_dim.105
  13.1 1.9 reshape.128
  15.1 0.5 fusion.12
  15.5 0.1 pad_maximum_fusion
  15.7 0.0 copy-done.1
  15.7 104.7 %while.24 = (s32[]{:T(128)}, f32[4,64,8192]{2,1,0:T(8,128)}, s32[4,2,512,64]{2,1,3,0:T(2,128)}, bf16[2,512,64]{2,1,0:T(8,128)(2,1)S(1)}, s32[]{:T(128)}, /*index=5*/s32[]{:T(128)}, s32[]{:T(128)}, s32[]{:T(128)}) while((s32[]{:T(128)}, f32[4,64,8192]{2,1,0:T(8,128)}, s32[4,2,512,64]{2,1,3,0:T(2,128)}, ...), condition=%wide.region_7.8_spmd.clone, body=%wide.region_4.7_spmd.clone.sunk | while | flops 542113792 | bytes 18351864 | solution.py:63
  15.7 1.0 constant_dynamic-slice_fusion.2
  16.7 0.2 copy.31
  16.9 23.5 %while.25 = (s32[]{:T(128)}, f32[64,8192]{1,0:T(8,128)S(1)}, bf16[2,512,64]{2,1,0:T(8,128)(2,1)S(1)}, s32[2,512,64]{2,1,0:T(8,128)S(1)}, s32[128]{0:T(128)S(1)}, /*index=5*/s32[]{:T(128)}, s32[]{:T(128)}) while((s32[]{:T(128)}, f32[64,8192]{1,0:T(8,128)S(1)}, bf16[2,512,64]{2,1,0:T(8,128)(2,1)S(1)}, s32[2,512,64]{2,1,0:T(8,128)S(1)}, ...), condition=%wide.region_6.6_spmd.clone, body=%wide.region_5.5_spmd.clone.sunk | while | flops 542113792 | bytes 13107807 | solution.py:60
  17.0 6.4 %broadcast_compare_fusion.2 = pred[512,64,128]{2,1,0:T(32,128)(4,1)} fusion(s32[128]{0:T(128)S(1)} %get-tuple-element.227, s32[512,64]{1,0:T(8,128)S(1)} %dynamic-slice_bitcast_fusion.2), kind=kLoop, calls=%fused_computation.6.clone.1 | loop fusion | flops 4194304 | bytes 4325888 | tf_op jit(solution)/shard_map/while/body/eval_jaxpr/while/body/eval_jaxpr/eq | solution.py:52
  23.4 5.2 %fusion.26 = f32[64,8192]{1,0:T(8,128)S(1)} fusion(pred[64,8,64,128]{3,2,1,0:T(32,128)(4,1)} %bitcast.52, f32[64,8192]{1,0:T(8,128)S(1)} %get-tuple-element.217, pred[]{:T(512)S(6)} %compare.6, bf16[2,512,64]{2,1,0:T(8,128)(2,1)S(1)} %get-tuple-element.225, s32[]{:T(128)} %get-tuple-element.216), kind=kOutput, calls=%fused_computation.5.clone.1 | convolution fusion | flops 537919488 | bytes 8519685 | tf_op jit(solution)/shard_map/while/body/eval_jaxpr/while/body/eval_jaxpr/dot_general | solution.py:54
  28.7 6.4 %broadcast_compare_fusion.2 = pred[512,64,128]{2,1,0:T(32,128)(4,1)} fusion(s32[128]{0:T(128)S(1)} %get-tuple-element.227, s32[512,64]{1,0:T(8,128)S(1)} %dynamic-slice_bitcast_fusion.2), kind=kLoop, calls=%fused_computation.6.clone.1 | loop fusion | flops 4194304 | bytes 4325888 | tf_op jit(solution)/shard_map/while/body/eval_jaxpr/while/body/eval_jaxpr/eq | solution.py:52
  35.1 5.2 %fusion.26 = f32[64,8192]{1,0:T(8,128)S(1)} fusion(pred[64,8,64,128]{3,2,1,0:T(32,128)(4,1)} %bitcast.52, f32[64,8192]{1,0:T(8,128)S(1)} %get-tuple-element.217, pred[]{:T(512)S(6)} %compare.6, bf16[2,512,64]{2,1,0:T(8,128)(2,1)S(1)} %get-tuple-element.225, s32[]{:T(128)} %get-tuple-element.216), kind=kOutput, calls=%fused_computation.5.clone.1 | convolution fusion | flops 537919488 | bytes 8519685 | tf_op jit(solution)/shard_map/while/body/eval_jaxpr/while/body/eval_jaxpr/dot_general | solution.py:54
  40.4 1.5 bitcast_dynamic-update-slice_fusion.2
  41.9 1.0 constant_dynamic-slice_fusion.2
  42.9 0.2 copy.31
  43.1 23.5 %while.25 = (s32[]{:T(128)}, f32[64,8192]{1,0:T(8,128)S(1)}, bf16[2,512,64]{2,1,0:T(8,128)(2,1)S(1)}, s32[2,512,64]{2,1,0:T(8,128)S(1)}, s32[128]{0:T(128)S(1)}, /*index=5*/s32[]{:T(128)}, s32[]{:T(128)}) while((s32[]{:T(128)}, f32[64,8192]{1,0:T(8,128)S(1)}, bf16[2,512,64]{2,1,0:T(8,128)(2,1)S(1)}, s32[2,512,64]{2,1,0:T(8,128)S(1)}, ...), condition=%wide.region_6.6_spmd.clone, body=%wide.region_5.5_spmd.clone.sunk | while | flops 542113792 | bytes 13107807 | solution.py:60
  43.2 6.4 %broadcast_compare_fusion.2 = pred[512,64,128]{2,1,0:T(32,128)(4,1)} fusion(s32[128]{0:T(128)S(1)} %get-tuple-element.227, s32[512,64]{1,0:T(8,128)S(1)} %dynamic-slice_bitcast_fusion.2), kind=kLoop, calls=%fused_computation.6.clone.1 | loop fusion | flops 4194304 | bytes 4325888 | tf_op jit(solution)/shard_map/while/body/eval_jaxpr/while/body/eval_jaxpr/eq | solution.py:52
  49.6 5.2 %fusion.26 = f32[64,8192]{1,0:T(8,128)S(1)} fusion(pred[64,8,64,128]{3,2,1,0:T(32,128)(4,1)} %bitcast.52, f32[64,8192]{1,0:T(8,128)S(1)} %get-tuple-element.217, pred[]{:T(512)S(6)} %compare.6, bf16[2,512,64]{2,1,0:T(8,128)(2,1)S(1)} %get-tuple-element.225, s32[]{:T(128)} %get-tuple-element.216), kind=kOutput, calls=%fused_computation.5.clone.1 | convolution fusion | flops 537919488 | bytes 8519685 | tf_op jit(solution)/shard_map/while/body/eval_jaxpr/while/body/eval_jaxpr/dot_general | solution.py:54
  54.9 6.4 %broadcast_compare_fusion.2 = pred[512,64,128]{2,1,0:T(32,128)(4,1)} fusion(s32[128]{0:T(128)S(1)} %get-tuple-element.227, s32[512,64]{1,0:T(8,128)S(1)} %dynamic-slice_bitcast_fusion.2), kind=kLoop, calls=%fused_computation.6.clone.1 | loop fusion | flops 4194304 | bytes 4325888 | tf_op jit(solution)/shard_map/while/body/eval_jaxpr/while/body/eval_jaxpr/eq | solution.py:52
  61.3 5.2 %fusion.26 = f32[64,8192]{1,0:T(8,128)S(1)} fusion(pred[64,8,64,128]{3,2,1,0:T(32,128)(4,1)} %bitcast.52, f32[64,8192]{1,0:T(8,128)S(1)} %get-tuple-element.217, pred[]{:T(512)S(6)} %compare.6, bf16[2,512,64]{2,1,0:T(8,128)(2,1)S(1)} %get-tuple-element.225, s32[]{:T(128)} %get-tuple-element.216), kind=kOutput, calls=%fused_computation.5.clone.1 | convolution fusion | flops 537919488 | bytes 8519685 | tf_op jit(solution)/shard_map/while/body/eval_jaxpr/while/body/eval_jaxpr/dot_general | solution.py:54
  66.6 1.5 bitcast_dynamic-update-slice_fusion.2
  68.0 1.0 constant_dynamic-slice_fusion.2
  69.0 0.2 copy.31
  69.2 23.5 %while.25 = (s32[]{:T(128)}, f32[64,8192]{1,0:T(8,128)S(1)}, bf16[2,512,64]{2,1,0:T(8,128)(2,1)S(1)}, s32[2,512,64]{2,1,0:T(8,128)S(1)}, s32[128]{0:T(128)S(1)}, /*index=5*/s32[]{:T(128)}, s32[]{:T(128)}) while((s32[]{:T(128)}, f32[64,8192]{1,0:T(8,128)S(1)}, bf16[2,512,64]{2,1,0:T(8,128)(2,1)S(1)}, s32[2,512,64]{2,1,0:T(8,128)S(1)}, ...), condition=%wide.region_6.6_spmd.clone, body=%wide.region_5.5_spmd.clone.sunk | while | flops 542113792 | bytes 13107807 | solution.py:60
  69.3 6.4 %broadcast_compare_fusion.2 = pred[512,64,128]{2,1,0:T(32,128)(4,1)} fusion(s32[128]{0:T(128)S(1)} %get-tuple-element.227, s32[512,64]{1,0:T(8,128)S(1)} %dynamic-slice_bitcast_fusion.2), kind=kLoop, calls=%fused_computation.6.clone.1 | loop fusion | flops 4194304 | bytes 4325888 | tf_op jit(solution)/shard_map/while/body/eval_jaxpr/while/body/eval_jaxpr/eq | solution.py:52
  75.7 5.2 %fusion.26 = f32[64,8192]{1,0:T(8,128)S(1)} fusion(pred[64,8,64,128]{3,2,1,0:T(32,128)(4,1)} %bitcast.52, f32[64,8192]{1,0:T(8,128)S(1)} %get-tuple-element.217, pred[]{:T(512)S(6)} %compare.6, bf16[2,512,64]{2,1,0:T(8,128)(2,1)S(1)} %get-tuple-element.225, s32[]{:T(128)} %get-tuple-element.216), kind=kOutput, calls=%fused_computation.5.clone.1 | convolution fusion | flops 537919488 | bytes 8519685 | tf_op jit(solution)/shard_map/while/body/eval_jaxpr/while/body/eval_jaxpr/dot_general | solution.py:54
  81.0 6.4 %broadcast_compare_fusion.2 = pred[512,64,128]{2,1,0:T(32,128)(4,1)} fusion(s32[128]{0:T(128)S(1)} %get-tuple-element.227, s32[512,64]{1,0:T(8,128)S(1)} %dynamic-slice_bitcast_fusion.2), kind=kLoop, calls=%fused_computation.6.clone.1 | loop fusion | flops 4194304 | bytes 4325888 | tf_op jit(solution)/shard_map/while/body/eval_jaxpr/while/body/eval_jaxpr/eq | solution.py:52
  87.5 5.2 %fusion.26 = f32[64,8192]{1,0:T(8,128)S(1)} fusion(pred[64,8,64,128]{3,2,1,0:T(32,128)(4,1)} %bitcast.52, f32[64,8192]{1,0:T(8,128)S(1)} %get-tuple-element.217, pred[]{:T(512)S(6)} %compare.6, bf16[2,512,64]{2,1,0:T(8,128)(2,1)S(1)} %get-tuple-element.225, s32[]{:T(128)} %get-tuple-element.216), kind=kOutput, calls=%fused_computation.5.clone.1 | convolution fusion | flops 537919488 | bytes 8519685 | tf_op jit(solution)/shard_map/while/body/eval_jaxpr/while/body/eval_jaxpr/dot_general | solution.py:54
  92.7 1.5 bitcast_dynamic-update-slice_fusion.2
  94.2 1.0 constant_dynamic-slice_fusion.2
  95.2 0.2 copy.31
  95.4 23.5 %while.25 = (s32[]{:T(128)}, f32[64,8192]{1,0:T(8,128)S(1)}, bf16[2,512,64]{2,1,0:T(8,128)(2,1)S(1)}, s32[2,512,64]{2,1,0:T(8,128)S(1)}, s32[128]{0:T(128)S(1)}, /*index=5*/s32[]{:T(128)}, s32[]{:T(128)}) while((s32[]{:T(128)}, f32[64,8192]{1,0:T(8,128)S(1)}, bf16[2,512,64]{2,1,0:T(8,128)(2,1)S(1)}, s32[2,512,64]{2,1,0:T(8,128)S(1)}, ...), condition=%wide.region_6.6_spmd.clone, body=%wide.region_5.5_spmd.clone.sunk | while | flops 542113792 | bytes 13107807 | solution.py:60
  95.5 6.4 %broadcast_compare_fusion.2 = pred[512,64,128]{2,1,0:T(32,128)(4,1)} fusion(s32[128]{0:T(128)S(1)} %get-tuple-element.227, s32[512,64]{1,0:T(8,128)S(1)} %dynamic-slice_bitcast_fusion.2), kind=kLoop, calls=%fused_computation.6.clone.1 | loop fusion | flops 4194304 | bytes 4325888 | tf_op jit(solution)/shard_map/while/body/eval_jaxpr/while/body/eval_jaxpr/eq | solution.py:52
  101.9 5.2 %fusion.26 = f32[64,8192]{1,0:T(8,128)S(1)} fusion(pred[64,8,64,128]{3,2,1,0:T(32,128)(4,1)} %bitcast.52, f32[64,8192]{1,0:T(8,128)S(1)} %get-tuple-element.217, pred[]{:T(512)S(6)} %compare.6, bf16[2,512,64]{2,1,0:T(8,128)(2,1)S(1)} %get-tuple-element.225, s32[]{:T(128)} %get-tuple-element.216), kind=kOutput, calls=%fused_computation.5.clone.1 | convolution fusion | flops 537919488 | bytes 8519685 | tf_op jit(solution)/shard_map/while/body/eval_jaxpr/while/body/eval_jaxpr/dot_general | solution.py:54
  107.2 6.4 %broadcast_compare_fusion.2 = pred[512,64,128]{2,1,0:T(32,128)(4,1)} fusion(s32[128]{0:T(128)S(1)} %get-tuple-element.227, s32[512,64]{1,0:T(8,128)S(1)} %dynamic-slice_bitcast_fusion.2), kind=kLoop, calls=%fused_computation.6.clone.1 | loop fusion | flops 4194304 | bytes 4325888 | tf_op jit(solution)/shard_map/while/body/eval_jaxpr/while/body/eval_jaxpr/eq | solution.py:52
  113.6 5.2 %fusion.26 = f32[64,8192]{1,0:T(8,128)S(1)} fusion(pred[64,8,64,128]{3,2,1,0:T(32,128)(4,1)} %bitcast.52, f32[64,8192]{1,0:T(8,128)S(1)} %get-tuple-element.217, pred[]{:T(512)S(6)} %compare.6, bf16[2,512,64]{2,1,0:T(8,128)(2,1)S(1)} %get-tuple-element.225, s32[]{:T(128)} %get-tuple-element.216), kind=kOutput, calls=%fused_computation.5.clone.1 | convolution fusion | flops 537919488 | bytes 8519685 | tf_op jit(solution)/shard_map/while/body/eval_jaxpr/while/body/eval_jaxpr/dot_general | solution.py:54
  118.9 1.5 bitcast_dynamic-update-slice_fusion.2
  120.4 0.0 copy-start
  120.4 8.2 %copy.22 = f32[32,8,64,128]{3,2,1,0:T(8,128)} copy(f32[32,8,64,128]{3,1,2,0:T(8,128)} %bitcast.57) | data formatting | bytes 16777216
  128.6 0.0 copy-done
  128.7 133.9 %gather_fusion = f32[8192,128]{1,0:T(8,128)} fusion(f32[4,2,32,64,128]{4,3,2,1,0:T(8,128)} %bitcast.54, s32[8192]{0:T(1024)S(1)} %bitcast.53), kind=kCustom, calls=%fused_computation | custom fusion | bytes 8519680 | tf_op jit(solution)/shard_map/gather | solution.py:69
  262.5 2.6 copy.18
  265.1 98.3 %all_to_all.5 = f32[2,32,8,16,128]{4,3,1,0,2:T(8,128)S(1)} all-to-all(f32[2,32,8,16,128]{4,3,1,0,2:T(8,128)S(1)} %copy.18), channel_id=1, replica_groups=mesh['rows'=8,'rep'=4] {'rows'}, dimensions={2} | all-to-all | bytes 8388608 | tf_op jit(solution)/shard_map/all_to_all | solution.py:73
  363.5 0.3 fusion.19
  363.8 18.1 %reduce_window_sum.11 = f32[2,32,16,128]{3,2,1,0:T(8,128)S(1)} reduce-window(f32[2,32,16,128]{3,2,1,0:T(8,128)S(1)} %get-tuple-element.111, f32[]{:T(128)} %constant.49.clone.1), window={size=1x1x1x128 pad=0_0x0_0x0_0x127_0}, to_apply=%region_9.10 | reduce-window | flops 16646144 | bytes 1048580 | tf_op jit(solution)/shard_map/jit(cumsum)/reduce_window_sum | solution.py:78
  381.9 0.8 fusion.20
  382.7 0.7 copy.19
  383.3 38.8 %pmax.15 = f32[32]{0:T(128)} all-reduce(f32[32]{0:T(128)S(1)} %get-tuple-element.112), channel_id=1, replica_groups=mesh['rows'=8,'rep'=4] {'rows','rep'}, use_global_device_ids=true, to_apply=%region_13.14 | all-reduce | flops 32 | bytes 256 | tf_op jit(solution)/shard_map/pmax | solution.py:88
  (24 shorter events, 0.3 us)
Async XLA Ops:
  11.7 4.0 copy-start.1
  120.4 8.2 %copy-start = (s32[32,128]{1,0:T(8,128)S(1)}, s32[32,128]{1,0:T(8,128)}, u32[]{:S(2)}) copy-start(s32[32,128]{1,0:T(8,128)} %param.17) | copy-start | bytes 49156
where the time goes:
time: 423 us; the launch traced here: 422 us
  local copies, waits for them, and re-layouts  161 us (38%)
  blocking collectives  144 us (34%)
  other arithmetic  74.5 us (18%)
  matrix products  41.8 us (10%)
    gather x1, local copies, waits for them, and re-layouts, body(): selected = block_sums[block_of, channel, node_of, inner_of]  134 us
    all_to_all x1, blocking collectives, body(): lax.all_to_all(sectioned, 'rows', split_axis=2, concat_axis=2, tiled=True)  98.3 us
    eq x8, other arithmetic, add_rows(): one_hot = (piece[:, :, None] == bin_ids[None, None, :]).astype(jnp.bfloat16)  51.6 us
    dot_general x8, matrix products, add_rows(): lax.dot_general(weight_piece, one_hot, (((0,), (0,)), ((), ())), preferre...  41.8 us
    pmax x1, blocking collectives, body(): node_best = lax.pmax(node_local, ('rows', 'rep'))  38.8 us
    another operation x1, other arithmetic, body(): left_sums = jnp.cumsum(summed, axis=3)[:, :, :, :-1]  18.1 us
    unnamed x7, local copies, waits for them, and re-layouts  10.5 us

commit v1 on v0

v1 whole, which is shorter than its diff:
```python
import functools

import jax
import jax.numpy as jnp
from jax import lax
from jax.experimental import pallas as pl
from jax.experimental.pallas import tpu as pltpu
from jax.sharding import PartitionSpec as P

BINS = 128
LANES = 128
MESH = pl.DeviceIdType.MESH

l2_penalty = 1.0


def kernel(
    n_rows, n_rep,
    split_feature, split_bin, binned, gh, parents, elected,
    new_nodes, best_out, node_best,
    side_snd, side_rcv, bins_snd, bins_rcv, node_rcv, gh_rcv, le, acc, top_snd, top_rcv, all_snd, all_rcv,
    side_ss, side_rs, gh_ss, gh_rs, node_ss, node_rs, bins_ss, bins_rs, top_ss, top_rs, all_ss, all_rs,
):
    rows_here, block_width = binned.shape
    node_count, slots_here = elected.shape
    parent_count = split_feature.shape[0]
    owned = slots_here // n_rows
    me = lax.axis_index("rows")
    rep = lax.axis_index("rep")

    def at_row(d):
        return (lax.rem(me + d, n_rows), rep)

    def at_rep(d):
        return (me, lax.rem(rep + d, n_rep))

    def send(src, dst, ss, rs, device):
        copy = pltpu.make_async_remote_copy(
            src_ref=src, dst_ref=dst, send_sem=ss, recv_sem=rs, device_id=device, device_id_type=MESH
        )
        copy.start()
        return copy

    barrier = pltpu.get_barrier_semaphore()
    for d in range(1, n_rep):
        pl.semaphore_signal(barrier, inc=1, device_id=at_rep(d), device_id_type=MESH)
    for d in range(1, n_rows):
        pl.semaphore_signal(barrier, inc=1, device_id=at_row(d), device_id_type=MESH)

    parent_sub = lax.broadcasted_iota(jnp.int32, (parent_count, block_width), 0)
    column = lax.broadcasted_iota(jnp.int32, (parent_count, block_width), 1) + rep * block_width
    feature_of = jnp.zeros((parent_count, block_width), jnp.int32)
    parent_row = lax.broadcasted_iota(jnp.int32, (parent_count, rows_here), 0)
    bin_of = jnp.zeros((parent_count, rows_here), jnp.int32)
    owns = jnp.zeros((parent_count, rows_here), jnp.int32)
    low = rep * block_width
    for p in range(parent_count):
        feature = split_feature[p]
        owned_here = jnp.where((feature >= low) & (feature < low + block_width), 1, 0)
        feature_of = jnp.where(parent_sub == p, feature, feature_of)
        bin_of = jnp.where(parent_row == p, split_bin[p], bin_of)
        owns = jnp.where(parent_row == p, owned_here, owns)
    picks = jnp.where(feature_of == column, 1.0, 0.0).astype(jnp.bfloat16)
    values = lax.dot_general(
        picks,
        binned[...].astype(jnp.float32).astype(jnp.bfloat16),
        (((1,), (1,)), ((), ())),
        preferred_element_type=jnp.float32,
    )
    own_parents = parents[...]
    goes = (parent_row == own_parents) & (owns > 0) & (values > bin_of.astype(jnp.float32))
    side = jnp.sum(jnp.where(goes, 1.0, 0.0), axis=0, keepdims=True)
    side_snd[...] = side

    pl.semaphore_wait(barrier, n_rep + n_rows - 2)
    copies = []
    for d in range(1, n_rep):
        copies.append(send(side_snd, side_rcv.at[d], side_ss.at[d], side_rs.at[d], at_rep(d)))
    for d in range(1, n_rows):
        copies.append(send(gh, gh_rcv.at[d], gh_ss.at[d], gh_rs.at[d], at_row(d)))
    gh_rcv[0] = gh[...]
    for d in range(1, n_rep):
        copies[d - 1].wait_recv()
        side = side + side_rcv[d]
    nodes = 2 * own_parents + side.astype(jnp.int32)
    new_nodes[...] = nodes
    node_rcv[0] = nodes

    node_sub = lax.broadcasted_iota(jnp.int32, (node_count, rows_here), 0)
    node_hot = jnp.where(node_sub == nodes, 1.0, 0.0).astype(jnp.bfloat16)
    index = lax.dot_general(
        node_hot,
        elected[...].astype(jnp.float32).astype(jnp.bfloat16),
        (((0,), (0,)), ((), ())),
        preferred_element_type=jnp.float32,
    ).astype(jnp.int32)
    lane = index % LANES
    part = index // LANES
    chosen = None
    for start in range(block_width // LANES):
        piece = binned[:, start * LANES : (start + 1) * LANES]
        found = jnp.take_along_axis(piece, lane, axis=1, mode="promise_in_bounds")
        chosen = found if chosen is None else jnp.where(part == start, found, chosen)
    turned = chosen.astype(jnp.float32).T
    for j in range(n_rows):
        bins_snd[j] = turned[j * owned : (j + 1) * owned]
    for d in range(1, n_rows):
        send(node_rcv.at[0], node_rcv.at[d], node_ss.at[d], node_rs.at[d], at_row(d))
        send(bins_snd.at[lax.rem(me + d, n_rows)], bins_rcv.at[d], bins_ss.at[d], bins_rs.at[d], at_row(d))
    bins_rcv[0] = bins_snd[me]

    def wait_for(d):
        for src, dst, ss, rs in (
            (gh, gh_rcv, gh_ss, gh_rs),
            (node_rcv.at[0], node_rcv, node_ss, node_rs),
            (bins_snd.at[0], bins_rcv, bins_ss, bins_rs),
        ):
            pltpu.make_async_remote_copy(
                src_ref=src, dst_ref=dst.at[d], send_sem=ss.at[d], recv_sem=rs.at[d],
                device_id=at_row(d), device_id_type=MESH,
            ).wait()

    bin_sub = lax.broadcasted_iota(jnp.int32, (BINS, rows_here), 0).astype(jnp.float32).astype(jnp.bfloat16)

    def add_source(d):
        there = node_sub == node_rcv[d]
        weights = jnp.concatenate(
            [jnp.where(there, gh_rcv[d, 0:1], 0.0), jnp.where(there, gh_rcv[d, 1:2], 0.0)], axis=0
        ).astype(jnp.bfloat16)
        bins = bins_rcv[d].astype(jnp.bfloat16)
        one = jnp.ones((), jnp.bfloat16)
        none = jnp.zeros((), jnp.bfloat16)
        for k in range(owned):
            le[k * BINS : (k + 1) * BINS, :] = jnp.where(bins[k : k + 1] <= bin_sub, one, none)
        return lax.dot_general(le[...], weights, (((1,), (1,)), ((), ())), preferred_element_type=jnp.float32)

    acc[...] = add_source(0)

    @pl.loop(1, n_rows)
    def _(d):
        wait_for(d)
        acc[...] += add_source(d)

    below = lax.broadcasted_iota(jnp.int32, (BINS, node_count), 0) < BINS - 1
    best = None
    for k in range(owned):
        left_grad = acc[k * BINS : (k + 1) * BINS, 0:node_count]
        left_hess = acc[k * BINS : (k + 1) * BINS, node_count : 2 * node_count]
        total_grad = left_grad[BINS - 1 : BINS]
        total_hess = left_hess[BINS - 1 : BINS]
        right_grad = total_grad - left_grad
        gain = 0.5 * (
            left_grad * left_grad / (left_hess + l2_penalty)
            + right_grad * right_grad / (total_hess - left_hess + l2_penalty)
            - total_grad * total_grad / (total_hess + l2_penalty)
        )
        top = jnp.max(jnp.where(below, gain, -jnp.inf), axis=0, keepdims=True)
        best_out[k : k + 1, :] = top
        best = top if best is None else jnp.maximum(best, top)

    def share(snd, rcv, ss, rs, size, at, value):
        snd[...] = value
        sent = [send(snd, rcv.at[d], ss.at[d], rs.at[d], at(d)) for d in range(1, size)]
        for d in range(1, size):
            sent[d - 1].wait()
            value = jnp.maximum(value, rcv[d])
        return value

    best = share(top_snd, top_rcv, top_ss, top_rs, n_rows, at_row, best)
    best = share(all_snd, all_rcv, all_ss, all_rs, n_rep, at_rep, best)
    node_best[...] = best
    for d in range(1, n_rep):
        copies[d - 1].wait_send()


def body(n_rows, n_rep, binned, gradients, hessians, parents, split_feature, split_bin, elected):
    rows_here, block_width = binned.shape
    node_count, slots_here = elected.shape
    owned = slots_here // n_rows
    f32 = jnp.float32
    gh = jnp.stack([gradients, hessians]).astype(f32)
    vmem = pl.BlockSpec(memory_space=pltpu.VMEM)
    smem = pl.BlockSpec(memory_space=pltpu.SMEM)
    dma = pltpu.SemaphoreType.DMA
    new_nodes, best, node_best = pl.pallas_call(
        functools.partial(kernel, n_rows, n_rep),
        out_shape=(
            jax.ShapeDtypeStruct((1, rows_here), jnp.int32),
            jax.ShapeDtypeStruct((owned, node_count), f32),
            jax.ShapeDtypeStruct((1, node_count), f32),
        ),
        in_specs=[smem, smem, vmem, vmem, vmem, vmem],
        out_specs=(vmem, vmem, vmem),
        scratch_shapes=[
            pltpu.VMEM((1, rows_here), f32),
            pltpu.VMEM((n_rep, 1, rows_here), f32),
            pltpu.VMEM((n_rows, owned, rows_here), f32),
            pltpu.VMEM((n_rows, owned, rows_here), f32),
            pltpu.VMEM((n_rows, 1, rows_here), jnp.int32),
            pltpu.VMEM((n_rows, 2, rows_here), f32),
            pltpu.VMEM((owned * BINS, rows_here), jnp.bfloat16),
            pltpu.VMEM((owned * BINS, 2 * node_count), f32),
            pltpu.VMEM((1, node_count), f32),
            pltpu.VMEM((n_rows, 1, node_count), f32),
            pltpu.VMEM((1, node_count), f32),
            pltpu.VMEM((n_rep, 1, node_count), f32),
        ]
        + [dma((n_rep,))] * 2 + [dma((n_rows,))] * 8 + [dma((n_rep,))] * 2,
        compiler_params=pltpu.CompilerParams(collective_id=0, has_side_effects=True),
    )(split_feature, split_bin, binned, gh, parents.reshape(1, rows_here), elected)
    return (
        new_nodes.reshape(rows_here),
        best.T.reshape(node_count, 1, owned),
        node_best.reshape(node_count),
    )


def solution(mesh):
    return jax.shard_map(
        functools.partial(body, mesh.shape["rows"], mesh.shape["rep"]),
        mesh=mesh,
        in_specs=(P("rows", "rep"), P("rows"), P("rows"), P("rows"), P(), P(), P(None, "rep")),
        out_specs=(P("rows"), P(None, "rep", "rows"), P()),
        check_vma=False,
    )
```

time: 423 us -> 43 us (0.10)
  local copies, waits for them, and re-layouts: 161 us -> 3.16 us
  blocking collectives: 144 us -> 0 us
  other arithmetic: 74.5 us -> 0.61 us
  matrix products: 41.8 us -> 0 us
  Pallas kernels: 0 us -> 38.3 us
    gather x1 -> x0, local copies, waits for them, and re-layouts: 134 us -> none  [body(): selected = block_sums[block_of, channel, node_of, inner_of]]
    all_to_all x1 -> x0, blocking collectives: 98.3 us -> none  [body(): lax.all_to_all(sectioned, 'rows', split_axis=2, concat_axis=2, tiled=True)]
    eq x8 -> x0, other arithmetic: 51.6 us -> none  [add_rows(): one_hot = (piece[:, :, None] == bin_ids[None, None, :]).astype(jnp.bfloat16)]
    pmax x2 -> x0, blocking collectives: 45.2 us -> none  [the longest x1 38.8 us: body(): node_best = lax.pmax(node_local, ('rows', 'rep'))]
    dot_general x8 -> x0, matrix products: 41.8 us -> none  [add_rows(): lax.dot_general(weight_piece, one_hot, (((0,), (0,)), ((), ())), preferre...]
    pallas_call x0 -> x1, Pallas kernels: none -> 38.3 us  [body(): pl.pallas_call(functools.partial(kernel, n_rows, n_rep), out_shape=(jax.S...]
    another operation x1 -> x0, other arithmetic: 18.1 us -> none  [body(): left_sums = jnp.cumsum(summed, axis=3)[:, :, :, :-1]]
    unnamed x7 -> x11, local copies, waits for them, and re-layouts: 10.5 us -> 2.46 us
where the time goes in v1:
time: 43 us; the launch traced here: 42.8 us
  Pallas kernels  38.3 us (89%)
  local copies, waits for them, and re-layouts  3.16 us (7%)
  between operations  0.67 us (2%)
  other arithmetic  0.61 us (1%)
    pallas_call x1, Pallas kernels, body(): pl.pallas_call(functools.partial(kernel, n_rows, n_rep), out_shape=(jax.S...  38.3 us
    unnamed x11, local copies, waits for them, and re-layouts  2.46 us

profile of v1, /device:TPU:0, one launch (start us, length us, event | category | flops | bytes accessed | tf_op | source)
XLA Modules:
  0.0 42.8 jit_solution(18220588541909965353)
XLA Ops:
  0.6 0.0 copy-start.2
  0.6 0.7 %stack.9 = bf16[1,1024]{1,0:T(2,128)(2,1)S(1)} reshape(bf16[1024]{0:T(1024)(128)(2,1)} %param.8) | data formatting | bytes 4096 | tf_op jit(solution)/shard_map/stack | solution.py:181
  1.3 0.0 copy-done.2
  1.3 0.6 %maximum_convert_fusion.gh = f32[2,1024]{1,0:T(2,128)} fusion(bf16[1,1024]{1,0:T(2,128)(2,1)S(1)} %stack.10, bf16[1,1024]{1,0:T(2,128)(2,1)S(1)} %stack.9), kind=kLoop, calls=%fused_computation | loop fusion | flops 8192 | bytes 12288 | tf_op jit(solution)/shard_map/convert_element_type | solution.py:181
  2.0 38.3 %shard_map.94 = (s32[1,1024]{1,0:T(1,128)}, f32[16,32]{1,0:T(8,128)}, f32[1,32]{1,0:T(1,128)}) custom-call(s32[16]{0:T(128)} %split_feature.1, s32[16]{0:T(128)} %split_bin.1, s32[1024,256]{1,0:T(8,128)} %binned.1, f32[2,1024]{1,0:T(2,128)} %maximum_convert_fusion.gh, s32[1,1024]{1,0:T(1,128)} %bitcast.7, s32[32,128]{1,0:T(8,128)} %elected.1), custom_call_target="tpu_custom_call" | custom-call | tf_op jit(solution)/shard_map/pallas_call | solution.py:185
  40.3 0.0 copy-start.1
  40.3 0.0 copy-start
  40.3 0.7 %copy-done.1 = s32[1,1024]{1,0:T(1,128)S(1)} copy-done((s32[1,1024]{1,0:T(1,128)S(1)}, s32[1,1024]{1,0:T(1,128)}, u32[]{:S(2)}) %copy-start.1) | copy-done | bytes 4120
  41.0 0.6 %copy.13 = s32[1024]{0:T(1024)} copy(s32[1024]{0:T(1024)S(1)} %bitcast.8) | data formatting | bytes 8192
  41.6 0.0 copy-done
  41.6 0.0 copy-start.3
  41.6 0.6 %copy.14 = f32[32,1,16]{0,2,1:T(8,128)} copy(f32[32,1,16]{0,2,1:T(8,128)S(1)} %bitcast.6) | data formatting | bytes 4096
  42.2 0.1 copy-done.3
  42.3 0.5 %copy.15 = f32[32]{0:T(128)} copy(f32[32]{0:T(128)S(1)} %bitcast.9) | data formatting | bytes 256
  (1 shorter events, 0.0 us)
Async XLA Ops:
  0.6 0.7 %copy-start.2 = (bf16[1024]{0:T(1024)(128)(2,1)S(1)}, bf16[1024]{0:T(1024)(128)(2,1)}, u32[]{:S(2)}) copy-start(bf16[1024]{0:T(1024)(128)(2,1)} %param.9) | copy-start | bytes 6148
  40.3 0.7 %copy-start.1 = (s32[1,1024]{1,0:T(1,128)S(1)}, s32[1,1024]{1,0:T(1,128)}, u32[]{:S(2)}) copy-start(s32[1,1024]{1,0:T(1,128)} %get-tuple-element.6) | copy-start | bytes 12292
  40.3 1.3 %copy-start = (f32[16,32]{1,0:T(8,128)S(1)}, f32[16,32]{1,0:T(8,128)}, u32[]{:S(2)}) copy-start(f32[16,32]{1,0:T(8,128)} %get-tuple-element.7) | copy-start | bytes 6148
  41.6 0.7 %copy-start.3 = (f32[1,32]{1,0:T(1,128)S(1)}, f32[1,32]{1,0:T(1,128)}, u32[]{:S(2)}) copy-start(f32[1,32]{1,0:T(1,128)} %get-tuple-element.8) | copy-start | bytes 388

commit v2 on v1

--- a/solution.py
+++ b/solution.py
@@ -16,8 +16,9 @@
 
 def kernel(
     n_rows, n_rep,
-    split_feature, split_bin, binned, gh, parents, elected,
+    split_feature_in, split_bin_in, binned_in, gradients_in, hessians_in, parents_in, elected_in,
     new_nodes, best_out, node_best,
+    split_feature, split_bin, binned, gradients, hessians, parents, elected, in_sems, gh, left_bins, right_bins,
     side_snd, side_rcv, bins_snd, bins_rcv, node_rcv, gh_rcv, le, acc, top_snd, top_rcv, all_snd, all_rcv,
     side_ss, side_rs, gh_ss, gh_rs, node_ss, node_rs, bins_ss, bins_rs, top_ss, top_rs, all_ss, all_rs,
 ):
@@ -28,8 +29,17 @@
     me = lax.axis_index("rows")
     rep = lax.axis_index("rep")
 
+    def partner(d):
+        if n_rows & (n_rows - 1):
+            return lax.rem(me + d, n_rows) if d else me
+        other = me
+        for bit in range(n_rows.bit_length()):
+            if d >> bit & 1:
+                other = other + (1 - 2 * lax.rem(me // 2**bit, 2)) * 2**bit
+        return other
+
     def at_row(d):
-        return (lax.rem(me + d, n_rows), rep)
+        return (partner(d), rep)
 
     def at_rep(d):
         return (me, lax.rem(rep + d, n_rep))
@@ -46,6 +56,20 @@
         pl.semaphore_signal(barrier, inc=1, device_id=at_rep(d), device_id_type=MESH)
     for d in range(1, n_rows):
         pl.semaphore_signal(barrier, inc=1, device_id=at_row(d), device_id_type=MESH)
+
+    loads = []
+    for i, (src, dst) in enumerate(
+        (
+            (binned_in, binned), (split_feature_in, split_feature), (split_bin_in, split_bin), (parents_in, parents),
+            (elected_in, elected), (gradients_in, gradients), (hessians_in, hessians),
+        )
+    ):
+        loads.append(pltpu.make_async_copy(src, dst, in_sems.at[i]))
+        loads[-1].start()
+    for load in loads:
+        load.wait()
+    gh[0:1] = gradients[...].astype(jnp.float32).reshape(1, rows_here)
+    gh[1:2] = hessians[...].astype(jnp.float32).reshape(1, rows_here)
 
     parent_sub = lax.broadcasted_iota(jnp.int32, (parent_count, block_width), 0)
     column = lax.broadcasted_iota(jnp.int32, (parent_count, block_width), 1) + rep * block_width
@@ -72,6 +96,22 @@
     side = jnp.sum(jnp.where(goes, 1.0, 0.0), axis=0, keepdims=True)
     side_snd[...] = side
 
+    node_sub = lax.broadcasted_iota(jnp.int32, (node_count, rows_here), 0)
+    elected_wide = elected[...].astype(jnp.float32).astype(jnp.bfloat16)
+    for child, turned in ((0, left_bins), (1, right_bins)):
+        child_hot = jnp.where(node_sub == 2 * own_parents + child, 1.0, 0.0).astype(jnp.bfloat16)
+        index = lax.dot_general(
+            child_hot, elected_wide, (((0,), (0,)), ((), ())), preferred_element_type=jnp.float32
+        ).astype(jnp.int32)
+        lane = index % LANES
+        part = index // LANES
+        chosen = None
+        for start in range(block_width // LANES):
+            piece = binned[:, start * LANES : (start + 1) * LANES]
+            found = jnp.take_along_axis(piece, lane, axis=1, mode="promise_in_bounds")
+            chosen = found if chosen is None else jnp.where(part == start, found, chosen)
+        turned[...] = chosen.astype(jnp.float32).T
+
     pl.semaphore_wait(barrier, n_rep + n_rows - 2)
     copies = []
     for d in range(1, n_rep):
@@ -86,27 +126,12 @@
     new_nodes[...] = nodes
     node_rcv[0] = nodes
 
-    node_sub = lax.broadcasted_iota(jnp.int32, (node_count, rows_here), 0)
-    node_hot = jnp.where(node_sub == nodes, 1.0, 0.0).astype(jnp.bfloat16)
-    index = lax.dot_general(
-        node_hot,
-        elected[...].astype(jnp.float32).astype(jnp.bfloat16),
-        (((0,), (0,)), ((), ())),
-        preferred_element_type=jnp.float32,
-    ).astype(jnp.int32)
-    lane = index % LANES
-    part = index // LANES
-    chosen = None
-    for start in range(block_width // LANES):
-        piece = binned[:, start * LANES : (start + 1) * LANES]
-        found = jnp.take_along_axis(piece, lane, axis=1, mode="promise_in_bounds")
-        chosen = found if chosen is None else jnp.where(part == start, found, chosen)
-    turned = chosen.astype(jnp.float32).T
     for j in range(n_rows):
-        bins_snd[j] = turned[j * owned : (j + 1) * owned]
+        slots = slice(j * owned, (j + 1) * owned)
+        bins_snd[j] = jnp.where(side > 0.5, right_bins[slots, :], left_bins[slots, :])
     for d in range(1, n_rows):
         send(node_rcv.at[0], node_rcv.at[d], node_ss.at[d], node_rs.at[d], at_row(d))
-        send(bins_snd.at[lax.rem(me + d, n_rows)], bins_rcv.at[d], bins_ss.at[d], bins_rs.at[d], at_row(d))
+        send(bins_snd.at[partner(d)], bins_rcv.at[d], bins_ss.at[d], bins_rs.at[d], at_row(d))
     bins_rcv[0] = bins_snd[me]
 
     def wait_for(d):
@@ -117,7 +142,7 @@
         ):
             pltpu.make_async_remote_copy(
                 src_ref=src, dst_ref=dst.at[d], send_sem=ss.at[d], recv_sem=rs.at[d],
-                device_id=at_row(d), device_id_type=MESH,
+                device_id=at_row(1), device_id_type=MESH,
             ).wait()
 
     bin_sub = lax.broadcasted_iota(jnp.int32, (BINS, rows_here), 0).astype(jnp.float32).astype(jnp.bfloat16)
@@ -173,14 +198,17 @@
         copies[d - 1].wait_send()
 
 
+def hand_on(*refs):
+    for src, dst in zip(refs[:3], refs[3:]):
+        dst[...] = src[...]
+
+
 def body(n_rows, n_rep, binned, gradients, hessians, parents, split_feature, split_bin, elected):
     rows_here, block_width = binned.shape
     node_count, slots_here = elected.shape
     owned = slots_here // n_rows
     f32 = jnp.float32
-    gh = jnp.stack([gradients, hessians]).astype(f32)
     vmem = pl.BlockSpec(memory_space=pltpu.VMEM)
-    smem = pl.BlockSpec(memory_space=pltpu.SMEM)
     dma = pltpu.SemaphoreType.DMA
     new_nodes, best, node_best = pl.pallas_call(
         functools.partial(kernel, n_rows, n_rep),
@@ -189,9 +217,20 @@
             jax.ShapeDtypeStruct((owned, node_count), f32),
             jax.ShapeDtypeStruct((1, node_count), f32),
         ),
-        in_specs=[smem, smem, vmem, vmem, vmem, vmem],
+        in_specs=[pl.BlockSpec(memory_space=pl.ANY)] * 7,
         out_specs=(vmem, vmem, vmem),
         scratch_shapes=[
+            pltpu.SMEM(split_feature.shape, jnp.int32),
+            pltpu.SMEM(split_bin.shape, jnp.int32),
+            pltpu.VMEM(binned.shape, jnp.int32),
+            pltpu.VMEM(gradients.shape, gradients.dtype),
+            pltpu.VMEM(hessians.shape, hessians.dtype),
+            pltpu.VMEM((1, rows_here), jnp.int32),
+            pltpu.VMEM(elected.shape, jnp.int32),
+            dma((7,)),
+            pltpu.VMEM((2, rows_here), f32),
+            pltpu.VMEM((slots_here, rows_here), f32),
+            pltpu.VMEM((slots_here, rows_here), f32),
             pltpu.VMEM((1, rows_here), f32),
             pltpu.VMEM((n_rep, 1, rows_here), f32),
             pltpu.VMEM((n_rows, owned, rows_here), f32),
@@ -207,7 +246,14 @@
         ]
         + [dma((n_rep,))] * 2 + [dma((n_rows,))] * 8 + [dma((n_rep,))] * 2,
         compiler_params=pltpu.CompilerParams(collective_id=0, has_side_effects=True),
-    )(split_feature, split_bin, binned, gh, parents.reshape(1, rows_here), elected)
+    )(split_feature, split_bin, binned, gradients, hessians, parents.reshape(1, rows_here), elected)
+    made = (new_nodes, best, node_best)
+    new_nodes, best, node_best = pl.pallas_call(
+        hand_on,
+        out_shape=tuple(jax.ShapeDtypeStruct(a.shape, a.dtype) for a in made),
+        in_specs=[vmem] * 3,
+        out_specs=(vmem,) * 3,
+    )(*made)
     return (
         new_nodes.reshape(rows_here),
         best.T.reshape(node_count, 1, owned),

time: 43 us -> 35.1 us (0.82)
  Pallas kernels: 38.3 us -> 34.3 us
  local copies, waits for them, and re-layouts: 3.16 us -> 0 us
  other arithmetic: 0.61 us -> 0 us
    pallas_call x1, Pallas kernels: 38.3 us -> 33 us  [body(): pl.pallas_call(functools.partial(kernel, n_rows, n_rep), out_shape=(jax.S...]
    unnamed x11 -> x0, local copies, waits for them, and re-layouts: 2.46 us -> none
    pallas_call x0 -> x1, Pallas kernels: none -> 1.3 us  [body(): pl.pallas_call(hand_on, out_shape=tuple((jax.ShapeDtypeStruct(a.shape, a....]
    another operation x2 -> x0, local copies, waits for them, and re-layouts: 0.7 us -> none  [body(): gh = jnp.stack([gradients, hessians]).astype(f32)]
    convert_element_type x1 -> x0, other arithmetic: 0.61 us -> none  [body(): gh = jnp.stack([gradients, hessians]).astype(f32)]
where the time goes in v2:
time: 35.1 us; the launch traced here: 34.9 us
  Pallas kernels  34.3 us (98%)
  between operations  0.64 us (2%)
    pallas_call x1, Pallas kernels, body(): pl.pallas_call(functools.partial(kernel, n_rows, n_rep), out_shape=(jax.S...  33 us
    pallas_call x1, Pallas kernels, body(): pl.pallas_call(hand_on, out_shape=tuple((jax.ShapeDtypeStruct(a.shape, a....  1.3 us

profile of v2, /device:TPU:0, one launch (start us, length us, event | category | flops | bytes accessed | tf_op | source)
XLA Modules:
  0.0 34.9 jit_solution(16888579120068103628)
XLA Ops:
  0.6 33.0 %shard_map.94 = (s32[1,1024]{1,0:T(1,128)}, f32[16,32]{1,0:T(8,128)}, f32[1,32]{1,0:T(1,128)}) custom-call(s32[16]{0:T(128)} %split_feature_in.1, s32[16]{0:T(128)} %split_bin_in.1, s32[1024,256]{1,0:T(8,128)} %binned_in.1, bf16[1024]{0:T(1024)(128)(2,1)} %gradients_in.1, bf16[1024]{0:T(1024)(128)(2,1)} %hessians_in.1, s32[1,1024]{1,0:T(1,128)} %bitcast.6, ...), custom_call_target="tpu_custom_call" | custom-call | tf_op jit(solution)/shard_map/pallas_call | solution.py:213
  33.6 1.3 %shard_map.95 = (s32[1,1024]{1,0:T(1,128)}, f32[16,32]{1,0:T(8,128)}, f32[1,32]{1,0:T(1,128)}) custom-call(s32[1,1024]{1,0:T(1,128)} %get-tuple-element.9.refs_0_, f32[16,32]{1,0:T(8,128)} %get-tuple-element.10.refs_1_, f32[1,32]{1,0:T(1,128)} %get-tuple-element.11.refs_2_), custom_call_target="tpu_custom_call" | custom-call | tf_op jit(solution)/shard_map/pallas_call | solution.py:251

commit v3 on v2

--- a/solution.py
+++ b/solution.py
@@ -19,8 +19,8 @@
     split_feature_in, split_bin_in, binned_in, gradients_in, hessians_in, parents_in, elected_in,
     new_nodes, best_out, node_best,
     split_feature, split_bin, binned, gradients, hessians, parents, elected, in_sems, gh, left_bins, right_bins,
-    side_snd, side_rcv, bins_snd, bins_rcv, node_rcv, gh_rcv, le, acc, top_snd, top_rcv, all_snd, all_rcv,
-    side_ss, side_rs, gh_ss, gh_rs, node_ss, node_rs, bins_ss, bins_rs, top_ss, top_rs, all_ss, all_rs,
+    side_snd, side_rcv, bins_snd, bins_rcv, node_rcv, gh_rcv, le, acc, top_snd, top_rcv,
+    side_ss, side_rs, gh_ss, gh_rs, node_ss, node_rs, bins_ss, bins_rs, top_ss, top_rs,
 ):
     rows_here, block_width = binned.shape
     node_count, slots_here = elected.shape
@@ -52,10 +52,13 @@
         return copy
 
     barrier = pltpu.get_barrier_semaphore()
-    for d in range(1, n_rep):
-        pl.semaphore_signal(barrier, inc=1, device_id=at_rep(d), device_id_type=MESH)
-    for d in range(1, n_rows):
-        pl.semaphore_signal(barrier, inc=1, device_id=at_row(d), device_id_type=MESH)
+    others = [(d, e) for d in range(n_rows) for e in range(n_rep) if d or e]
+
+    def at(d, e):
+        return (partner(d), lax.rem(rep + e, n_rep))
+
+    for d, e in others:
+        pl.semaphore_signal(barrier, inc=1, device_id=at(d, e), device_id_type=MESH)
 
     loads = []
     for i, (src, dst) in enumerate(
@@ -112,7 +115,7 @@
             chosen = found if chosen is None else jnp.where(part == start, found, chosen)
         turned[...] = chosen.astype(jnp.float32).T
 
-    pl.semaphore_wait(barrier, n_rep + n_rows - 2)
+    pl.semaphore_wait(barrier, len(others))
     copies = []
     for d in range(1, n_rep):
         copies.append(send(side_snd, side_rcv.at[d], side_ss.at[d], side_rs.at[d], at_rep(d)))
@@ -183,16 +186,13 @@
         best_out[k : k + 1, :] = top
         best = top if best is None else jnp.maximum(best, top)
 
-    def share(snd, rcv, ss, rs, size, at, value):
-        snd[...] = value
-        sent = [send(snd, rcv.at[d], ss.at[d], rs.at[d], at(d)) for d in range(1, size)]
-        for d in range(1, size):
-            sent[d - 1].wait()
-            value = jnp.maximum(value, rcv[d])
-        return value
-
-    best = share(top_snd, top_rcv, top_ss, top_rs, n_rows, at_row, best)
-    best = share(all_snd, all_rcv, all_ss, all_rs, n_rep, at_rep, best)
+    top_snd[...] = best
+    sent = []
+    for i, (d, e) in enumerate(others):
+        sent.append(send(top_snd, top_rcv.at[i], top_ss.at[i], top_rs.at[i], at(d, e)))
+    for i, copy in enumerate(sent):
+        copy.wait()
+        best = jnp.maximum(best, top_rcv[i])
     node_best[...] = best
     for d in range(1, n_rep):
         copies[d - 1].wait_send()
@@ -240,11 +240,9 @@
             pltpu.VMEM((owned * BINS, rows_here), jnp.bfloat16),
             pltpu.VMEM((owned * BINS, 2 * node_count), f32),
             pltpu.VMEM((1, node_count), f32),
-            pltpu.VMEM((n_rows, 1, node_count), f32),
-            pltpu.VMEM((1, node_count), f32),
-            pltpu.VMEM((n_rep, 1, node_count), f32),
+            pltpu.VMEM((n_rows * n_rep - 1, 1, node_count), f32),
         ]
-        + [dma((n_rep,))] * 2 + [dma((n_rows,))] * 8 + [dma((n_rep,))] * 2,
+        + [dma((n_rep,))] * 2 + [dma((n_rows,))] * 6 + [dma((n_rows * n_rep - 1,))] * 2,
         compiler_params=pltpu.CompilerParams(collective_id=0, has_side_effects=True),
     )(split_feature, split_bin, binned, gradients, hessians, parents.reshape(1, rows_here), elected)
     made = (new_nodes, best, node_best)

time: 35.1 us -> 33.6 us (0.957)
  Pallas kernels: 34.3 us -> 32.7 us
    pallas_call x1, Pallas kernels: 33 us -> 31.4 us  [body(): pl.pallas_call(functools.partial(kernel, n_rows, n_rep), out_shape=(jax.S...]
where the time goes in v3:
time: 33.6 us; the launch traced here: 33.4 us
  Pallas kernels  32.7 us (97%)
  between operations  0.64 us (2%)
    pallas_call x1, Pallas kernels, body(): pl.pallas_call(functools.partial(kernel, n_rows, n_rep), out_shape=(jax.S...  31.4 us
    pallas_call x1, Pallas kernels, body(): pl.pallas_call(hand_on, out_shape=tuple((jax.ShapeDtypeStruct(a.shape, a....  1.3 us

profile of v3, /device:TPU:0, one launch (start us, length us, event | category | flops | bytes accessed | tf_op | source)
XLA Modules:
  0.0 33.4 jit_solution(15617617142703734)
XLA Ops:
  0.6 31.4 %shard_map.94 = (s32[1,1024]{1,0:T(1,128)}, f32[16,32]{1,0:T(8,128)}, f32[1,32]{1,0:T(1,128)}) custom-call(s32[16]{0:T(128)} %split_feature_in.1, s32[16]{0:T(128)} %split_bin_in.1, s32[1024,256]{1,0:T(8,128)} %binned_in.1, bf16[1024]{0:T(1024)(128)(2,1)} %gradients_in.1, bf16[1024]{0:T(1024)(128)(2,1)} %hessians_in.1, s32[1,1024]{1,0:T(1,128)} %bitcast.6, ...), custom_call_target="tpu_custom_call" | custom-call | tf_op jit(solution)/shard_map/pallas_call | solution.py:213
  32.1 1.3 %shard_map.95 = (s32[1,1024]{1,0:T(1,128)}, f32[16,32]{1,0:T(8,128)}, f32[1,32]{1,0:T(1,128)}) custom-call(s32[1,1024]{1,0:T(1,128)} %get-tuple-element.9.refs_0_, f32[16,32]{1,0:T(8,128)} %get-tuple-element.10.refs_1_, f32[1,32]{1,0:T(1,128)} %get-tuple-element.11.refs_2_), custom_call_target="tpu_custom_call" | custom-call | tf_op jit(solution)/shard_map/pallas_call | solution.py:249
